TPU v7x, 32 devices: a whole 2x2x4 slice. The times are simulated.
32 devices in a mesh: section: 4 (over y, x), dp: 8 (over z, core).
Axes of the slice: x: 2, y: 2, z: 4, core: 2. Of those that a mesh axis runs over, the one named last changes fastest.
Arguments:
- owner_table: int32 [4, 4], P('section'), may hold values from 0 to 3, each once within a row
- hidden_acts: bfloat16 [4, 1024, 2048], P('section', 'dp'), may hold values from -6 to 6
- sent_grad: bfloat16 [4, 1024, 512], P('section', 'dp'), may hold values from -0.25 to 0.25
Outputs:
- update: bfloat16 [4, 4, 512, 512], P('section')
Inputs may be any that keep to these rules, and one draw needn't show every extreme that they name: `owner_table`: each section's row is a permutation of 0 to 3.
All inputs are finite; a program needn't handle non-finite values.
Results may differ from a plain program's by a relative error of at most 0.0098.
Values may be sent and summed in bfloat16 or wider, within the bound.
No kernel may reach another device: no remote copies, remote signals or barrier semaphores. Data moves between devices by JAX's collectives and lax.ppermute only.
A program may use at most 64 MiB of HBM per device.

v0:
```python
import jax
import jax.numpy as jnp
from jax import lax
from jax.sharding import PartitionSpec as P

BLK = 512
ITERS = 2


def shifted_2(value, axis, steps):
    count = lax.axis_size(axis)
    pairs = [(source, (source + steps) % count) for source in range(count)]
    return lax.ppermute(value, axis, pairs)


def partner_2(block, axis, stride):
    count = lax.axis_size(axis)
    route = []
    for low in range(count):
        high = low | 1 << stride
        if high != low and high < count:
            route += [(low, high), (high, low)]
    return lax.ppermute(block, axis, route)


def inverse_root(gram):
    unit_matrix = jnp.eye(BLK, dtype=jnp.float32)
    shifted = gram + 1e-06 * unit_matrix
    norm_value = jnp.sqrt(jnp.sum(shifted * shifted))
    scaled = shifted / norm_value
    result = None
    for step_index in range(ITERS):
        factor = ((5.0 * unit_matrix - scaled) / 4.0).astype(jnp.bfloat16)
        if step_index == 0:
            result = factor
        else:
            result = jnp.dot(result, factor, preferred_element_type=jnp.float32).astype(
                jnp.bfloat16
            )
        if step_index + 1 < ITERS:
            square = jnp.dot(factor, factor, preferred_element_type=jnp.float32).astype(
                jnp.bfloat16
            )
            fourth = jnp.dot(square, square, preferred_element_type=jnp.float32).astype(
                jnp.bfloat16
            )
            scaled = jnp.dot(
                fourth, scaled.astype(jnp.bfloat16), preferred_element_type=jnp.float32
            )
    return result


def gram_rows(matrix):
    return lax.dot_general(
        matrix, matrix, (((1,), (1,)), ((), ())), preferred_element_type=jnp.float32
    )


def shards(owner_table, hidden_acts, sent_grad):
    owners_row = owner_table[0]
    block_count = owners_row.shape[0]
    replica_count = lax.axis_size("dp")
    group_size = replica_count // block_count
    row_count = BLK // group_size
    bit_count = group_size.bit_length() - 1
    my_index = lax.axis_index("dp")
    incoming = shifted_2(sent_grad[0], "section", -1)
    activations = hidden_acts[0]
    tokens = activations.shape[0]
    picked = jnp.take(activations.reshape(tokens, block_count, BLK), owners_row, axis=1)
    member = my_index % group_size
    offset = 0
    ordered = picked.reshape(tokens, block_count * BLK)
    summed = lax.psum_scatter(
        lax.dot_general(
            ordered, incoming, (((0,), (0,)), ((), ())), preferred_element_type=jnp.float32
        ),
        "dp",
        scatter_dimension=0,
        tiled=True,
    )
    owned_block = summed.astype(jnp.bfloat16)
    for bit_level in range(bit_count):
        partner = partner_2(owned_block, "dp", offset + bit_level)
        is_upper = member >> bit_level & 1 == 1
        owned_block = jnp.where(
            is_upper,
            jnp.concatenate([partner, owned_block], axis=0),
            jnp.concatenate([owned_block, partner], axis=0),
        )
    takes_right = member & 1 == 1
    operand = jnp.where(takes_right, owned_block.T, owned_block)
    own_root = inverse_root(gram_rows(operand))
    partner_root = partner_2(own_root, "dp", offset)
    left_root = jnp.where(takes_right, partner_root, own_root)
    right_root = jnp.where(takes_right, own_root, partner_root)
    left_rows = lax.dynamic_slice_in_dim(left_root, member * row_count, row_count, 0)
    projected = jnp.dot(left_rows, owned_block, preferred_element_type=jnp.float32).astype(
        jnp.bfloat16
    )
    my_update = jnp.dot(projected, right_root, preferred_element_type=jnp.float32).astype(
        jnp.bfloat16
    )
    gathered = lax.all_gather(my_update, "dp", axis=0, tiled=True)
    result_blocks = gathered.reshape(block_count, BLK, BLK)
    return result_blocks[None]


def solution(mesh):
    return jax.shard_map(
        shards,
        mesh=mesh,
        in_specs=(P("section", None), P("section", "dp", None), P("section", "dp", None)),
        out_specs=P("section", None, None, None),
        check_vma=False,
    )
```

profile of v0, /device:TPU:0, one launch (start us, length us, event | category | flops | bytes accessed | tf_op | source)
XLA Modules:
  0.0 116.2 jit_solution(1770904773357972307)
XLA Ops:
  6.5 0.0 reduce-scatter.2.cloned.1.call-start
  6.5 3.9 %collective-permute-start = (bf16[128,512]{1,0:T(8,128)(2,1)}, bf16[128,512]{1,0:T(8,128)(2,1)S(1)}, u32[]{:S(2)}, u32[]{:S(2)}) collective-permute-start(bf16[128,512]{1,0:T(8,128)(2,1)} %bitcast.28), channel_id=1, source_target_pairs={{0,24},{8,0},{16,8},{24,16},{1,25},{9,1},{17,9},{25,17},{2,26},{10... | collective-permute-start | bytes 393224 | tf_op jit(solution)/shard_map/ppermute | solution.py:13
  10.5 0.7 fusion.23
  11.1 0.7 compare_and_fusion
  11.8 1.3 %copy.6 = bf16[1,128,2048]{1,2,0:T(8,128)(2,1)S(1)} copy(bf16[1,128,2048]{2,1,0:T(8,128)(2,1)} %param.4) | data formatting | bytes 1048576 | tf_op args[1]
  13.1 0.2 copy.7
  13.3 0.6 gather_fusion
  13.9 0.3 copy.8
  14.2 0.1 broadcast_bitcast_fusion
  14.3 0.3 bitcast_select_fusion.2
  14.6 0.0 collective-permute-done
  14.6 2.6 %fusion.35 = f32[2048,512]{1,0:T(8,128)} fusion(bf16[128,2048]{0,1:T(8,128)(2,1)S(1)} %bitcast_select_fusion.2, bf16[128,512]{1,0:T(8,128)(2,1)S(1)} %collective-permute-done), kind=kOutput, calls=%fused_computation.44 | convolution fusion | flops 268435456 | bytes 4849664 | tf_op jit(solution)/shard_map/dot_general | solution.py:75
  17.3 0.0 reduce-scatter.2.cloned.1.call-update
  17.3 0.0 all-gather.2.cloned.1.call-start
  17.4 51.0 %reduce-scatter.2.cloned.1.call-done = f32[256,512]{1,0:T(8,128)} async-done(((f32[2048,512]{1,0:T(8,128)}), f32[256,512]{1,0:T(8,128)}) %reduce-scatter.2.cloned.1.call-update) | async-done | bytes 524304 | tf_op jit(solution)/shard_map/reduce_scatter | solution.py:74
  68.3 1.1 convert_element_type.28
  69.4 0.1 collective-permute-start.1
  69.5 1.5 %collective-permute-done.1 = bf16[256,512]{1,0:T(8,128)(2,1)S(1)} collective-permute-done((bf16[256,512]{1,0:T(8,128)(2,1)S(1)}, bf16[256,512]{1,0:T(8,128)(2,1)S(1)}, u32[]{:S(2)}, u32[]{:S(2)}) %collective-permute-start.1) | collective-permute-done | bytes 262176 | tf_op jit(solution)/shard_map/ppermute | solution.py:23
  71.0 0.2 maximum_select_fusion
  71.2 0.2 copy.9
  71.4 1.2 %multiply_reduce_fusion = (f32[]{:T(128)}, f32[512,512]{1,0:T(8,128)S(1)}) fusion(bf16[512,512]{1,0:T(8,128)(2,1)S(1)} %maximum_select_fusion, bf16[512,512]{0,1:T(8,128)(2,1)S(1)} %copy.9, pred[]{:T(512)S(6)} %eq.15), kind=kOutput, calls=%fused_computation.13 | convolution fusion | flops 270008320 | bytes 2097157 | tf_op jit(solution)/shard_map/dot_general | solution.py:54
  73.4 1.1 convolution_convert_fusion.1
  74.5 0.8 convolution_convert_fusion
  75.3 0.2 collective-permute-start.2
  75.5 1.8 %collective-permute-done.2 = bf16[512,512]{1,0:T(8,128)(2,1)S(1)} collective-permute-done((bf16[512,512]{1,0:T(8,128)(2,1)S(1)}, bf16[512,512]{1,0:T(8,128)(2,1)S(1)}, u32[]{:S(2)}, u32[]{:S(2)}) %collective-permute-start.2) | collective-permute-done | bytes 524320 | tf_op jit(solution)/shard_map/ppermute | solution.py:23
  77.3 1.2 %convolution_convert_fusion.3 = bf16[256,512]{1,0:T(8,128)(2,1)} fusion(bf16[512,512]{1,0:T(8,128)(2,1)S(1)} %maximum_select_fusion, bf16[512,512]{1,0:T(8,128)(2,1)S(1)} %convolution_convert_fusion, bf16[512,512]{1,0:T(8,128)(2,1)S(1)} %collective-permute-done.2, pred[]{:T(512)S(6)} %eq.15, s32[]{:T(128)S(6)} %select_n.62), kind=kOutput, calls=%fused_computation.9 | convolution fusion | flops 269090816 | bytes 2360832 | tf_op jit(solution)/shard_map/dot_general | solution.py:101
  78.5 0.0 all-gather.2.cloned.1.call-update
  78.5 27.8 %all-gather.2.cloned.1.call-done = bf16[2048,512]{1,0:T(8,128)(2,1)} async-done(((bf16[256,512]{1,0:T(8,128)(2,1)}), bf16[2048,512]{1,0:T(8,128)(2,1)}) %all-gather.2.cloned.1.call-update) | async-done | bytes 2097168 | tf_op jit(solution)/shard_map/all_gather | solution.py:104
  106.3 3.0 %copy.12 = bf16[1,4,512,512]{3,2,1,0:T(8,128)(2,1)} copy(bf16[1,4,512,512]{3,2,1,0:T(8,128)(2,1)} %bitcast.24) | data formatting | bytes 4194304
  (2 shorter events, 0.0 us)
Async XLA Ops:
  6.5 61.8 %reduce-scatter.2.cloned.1.call-start = ((), (), s32[]{:S(2)}) async-start(), calls=%async_computation.1 | async-start | bytes 4718592 | tf_op jit(solution)/shard_map/reduce_scatter | solution.py:74
  6.5 8.1 %collective-permute-start = (bf16[128,512]{1,0:T(8,128)(2,1)}, bf16[128,512]{1,0:T(8,128)(2,1)S(1)}, u32[]{:S(2)}, u32[]{:S(2)}) collective-permute-start(bf16[128,512]{1,0:T(8,128)(2,1)} %bitcast.28), channel_id=1, source_target_pairs={{0,24},{8,0},{16,8},{24,16},{1,25},{9,1},{17,9},{25,17},{2,26},{10... | collective-permute-start | bytes 393224 | tf_op jit(solution)/shard_map/ppermute | solution.py:13
  17.3 89.0 %all-gather.2.cloned.1.call-start = ((), (), s32[]{:S(2)}) async-start(), calls=%async_computation.2 | async-start | bytes 2359296 | tf_op jit(solution)/shard_map/all_gather | solution.py:104
  69.4 1.6 %collective-permute-start.1 = (bf16[256,512]{1,0:T(8,128)(2,1)S(1)}, bf16[256,512]{1,0:T(8,128)(2,1)S(1)}, u32[]{:S(2)}, u32[]{:S(2)}) collective-permute-start(bf16[256,512]{1,0:T(8,128)(2,1)S(1)} %convert_element_type.28), channel_id=1, source_target_pairs={{0,1},{1,0},{2,3},{3,2},{4,5},{5,4},{6,7},{7,6},{8,9},{9,8},{10,11... | collective-permute-start | bytes 786440 | tf_op jit(solution)/shard_map/ppermute | solution.py:23
  75.3 2.0 %collective-permute-start.2 = (bf16[512,512]{1,0:T(8,128)(2,1)S(1)}, bf16[512,512]{1,0:T(8,128)(2,1)S(1)}, u32[]{:S(2)}, u32[]{:S(2)}) collective-permute-start(bf16[512,512]{1,0:T(8,128)(2,1)S(1)} %convolution_convert_fusion), channel_id=1, source_target_pairs={{0,1},{1,0},{2,3},{3,2},{4,5},{5,4},{6,7},{7,6},{8,9},{9,8},{10,11... | collective-permute-start | bytes 1572872 | tf_op jit(solution)/shard_map/ppermute | solution.py:23
Sparse Core Ops, SparseCore 0:
  17.4 50.8 reduce-scatter.1
  78.6 27.6 all-gather.1
where the time goes:
time: 116 us
  waiting for transfers between devices  82.1 us (71%)
  between operations  14.2 us (12%)
  matrix products  6.98 us (6%)
  local copies, waits for them, and re-layouts  5.71 us (5%)
  starting transfers between devices  4.23 us (4%)
  other arithmetic  2.95 us (3%)
    reduce_scatter x1, waiting for transfers between devices, shards(): lax.psum_scatter(lax.dot_general(ordered, incoming, (((0,), (0,)), ((), (...  51 us
    all_gather x1, waiting for transfers between devices, shards(): gathered = lax.all_gather(my_update, 'dp', axis=0, tiled=True)  27.8 us
    unnamed x4, local copies, waits for them, and re-layouts  4.44 us
    ppermute x1, starting transfers between devices, shifted_2(): return lax.ppermute(value, axis, pairs)  3.92 us
    ppermute x2, waiting for transfers between devices, partner_2(): return lax.ppermute(block, axis, route)  3.29 us
    dot_general x1, matrix products, shards(): lax.dot_general(ordered, incoming, (((0,), (0,)), ((), ())), preferred_el...  2.63 us
  transfers between devices with their start and end apart: 5, of which 4 were waited for; matrix products, arithmetic and copies ran while one was open for 4% of the time, Pallas kernels for 0%

commit v1 on v0

--- a/solution.py
+++ b/solution.py
@@ -1,6 +1,10 @@
+import functools
+
 import jax
 import jax.numpy as jnp
 from jax import lax
+from jax.experimental import pallas as pl
+from jax.experimental.pallas import tpu as pltpu
 from jax.sharding import PartitionSpec as P
 
 BLK = 512
@@ -106,9 +110,228 @@
     return result_blocks[None]
 
 
+def matmul(left, right, dims=((1,), (0,))):
+    return lax.dot_general(left, right, (dims, ((), ())), preferred_element_type=jnp.float32)
+
+
+def spot():
+    return lax.axis_index("dp") // 2, lax.rem(lax.axis_index("dp"), 2)
+
+
+def line_route(count, origins, start, gap):
+    up = [(low + start, low + gap) for low in origins]
+    pairs = [(2 * a, 2 * b) for a, b in up]
+    return pairs + [(2 * (count - 1 - a) + 1, 2 * (count - 1 - b) + 1) for a, b in up]
+
+
+def line_hops(count):
+    half = count // 2
+    hops = [("far", range(count - half - 1), 0, half)]
+    hops += [("near", range(count - half - 1, count - half), 0, half)]
+    hops += [(f"by{gap}", range(count - gap), 0, gap) for gap in range(1, half)]
+    hops += [(f"on{gap}", range(count - gap), half, gap) for gap in range(half + 1, count)]
+    return [hop for hop in hops if len(hop[1])]
+
+
+def pick_kernel(count, first, table, acts, *refs):
+    where, core = spot()
+    *outs, owners, sem = refs
+    outs = outs[-count:]
+    tokens = acts.shape[0]
+    copy = pltpu.make_async_copy(table, owners, sem.at[0])
+    copy.start()
+    copy.wait()
+    width = outs[0].shape[1]
+    for gap, out in enumerate(outs):
+        target = jnp.clip(jnp.where(core == 0, where + gap, where - gap), 0, count - 1)
+        columns = pl.ds(pl.multiple_of(owners[0, target] * width, width), width)
+        out[0 if first else tokens : tokens if first else 2 * tokens] = acts[:, columns]
+
+
+def join_kernel(low, high, out):
+    out[: low.shape[0]] = low[...]
+    out[low.shape[0] :] = high[...]
+
+
+def unit_of(side):
+    rows = lax.broadcasted_iota(jnp.int32, (side, side), 0)
+    return (rows == lax.broadcasted_iota(jnp.int32, (side, side), 1)).astype(jnp.float32)
+
+
+def factor_of(scaled, unit):
+    return ((5.0 * unit - scaled) / 4.0).astype(jnp.bfloat16)
+
+
+def normalized(gram, unit):
+    shifted = gram + 1e-06 * unit
+    return shifted * (1.0 / jnp.sqrt(jnp.sum(shifted * shifted)))
+
+
+def update_kernel(terms, *refs):
+    *pieces, out_low, out_high = refs
+    total = None
+    for acts, grads in terms:
+        right = functools.reduce(lambda a, b: a + b, [pieces[at][...] for at in grads])
+        term = matmul(pieces[acts][...], right, ((0,), (0,)))
+        total = term if total is None else total + term
+    owned = total.astype(jnp.bfloat16)
+    flipped = owned.T
+    unit = unit_of(owned.shape[0])
+    scaled = [normalized(matmul(owned, flipped), unit), normalized(matmul(flipped, owned), unit)]
+    roots = None
+    for step_index in range(ITERS):
+        factors = [factor_of(term, unit) for term in scaled]
+        if step_index == 0:
+            roots = factors
+        else:
+            roots = [matmul(a, b).astype(jnp.bfloat16) for a, b in zip(roots, factors)]
+        if step_index + 1 < ITERS:
+            squares = [matmul(a, a).astype(jnp.bfloat16) for a in factors]
+            fourths = [matmul(a, a).astype(jnp.bfloat16) for a in squares]
+            scaled = [matmul(a, b.astype(jnp.bfloat16)) for a, b in zip(fourths, scaled)]
+    projected = matmul(roots[0], owned).astype(jnp.bfloat16)
+    update = matmul(projected, roots[1]).astype(jnp.bfloat16)
+    rows = out_low.shape[0]
+    out_low[...] = update[:rows]
+    out_high[...] = update[rows:]
+
+
+def place_kernel(count, jobs, *refs):
+    *pieces, out, sems = refs
+    where, core = spot()
+    rows = pieces[0].shape[0]
+    at = 0
+    copies = []
+    for origins, gap, part in jobs:
+        for mirrored in (False, True) if gap else (False,):
+            up = core == (1 if mirrored else 0)
+            block = jnp.where(up, where - gap, where + gap)
+            rank = jnp.where(up, block, count - 1 - block)
+            live = jnp.logical_and(rank >= origins[0], rank <= origins[-1])
+            target = out.at[jnp.clip(block, 0, count - 1), pl.ds(part * rows, rows)]
+            copies.append((live, pltpu.make_async_copy(pieces[at], target, sems.at[at])))
+            at += 1
+    for live, copy in copies:
+        pl.when(live)(copy.start)
+    for live, copy in copies:
+        pl.when(live)(copy.wait)
+
+
+VMEM = pl.BlockSpec(memory_space=pltpu.VMEM)
+IN_HBM = pl.BlockSpec(memory_space=pltpu.HBM)
+PARAMS = pltpu.CompilerParams(vmem_limit_bytes=24 * 2**20)
+
+
+def cost(flops, moved):
+    return pl.CostEstimate(flops=flops, bytes_accessed=moved, transcendentals=0)
+
+
+def pair_shards(owner_table, hidden_acts, sent_grad):
+    activations, outgoing = hidden_acts[0], sent_grad[0]
+    count = owner_table.shape[1]
+    tokens, width = outgoing.shape
+    sections, replicas = lax.axis_size("section"), lax.axis_size("dp")
+    swap_route = [(a, a ^ 1) for a in range(replicas)]
+
+    def swap(piece):
+        return lax.ppermute(piece, "dp", swap_route)
+
+    def along(piece, route):
+        return lax.ppermute(piece, "dp", route)
+
+    def relayed(piece, route):
+        pairs = [
+            ((s + 1) % sections * replicas + a, s * replicas + b)
+            for s in range(sections)
+            for a, b in route
+        ]
+        return lax.ppermute(piece, ("section", "dp"), pairs)
+
+    acts_other = swap(activations)
+    grads_other = swap(outgoing)
+    picked = ()
+    for first, part in ((True, activations), (False, acts_other)):
+        picked = pl.pallas_call(
+            functools.partial(pick_kernel, count, first),
+            out_shape=[jax.ShapeDtypeStruct((2 * tokens, BLK), activations.dtype)] * count,
+            in_specs=[IN_HBM, VMEM] + [VMEM] * len(picked),
+            out_specs=[VMEM] * count,
+            input_output_aliases={2 + at: at for at in range(len(picked))},
+            scratch_shapes=[
+                pltpu.SMEM(owner_table.shape, owner_table.dtype),
+                pltpu.SemaphoreType.DMA((1,)),
+            ],
+            compiler_params=PARAMS,
+            cost_estimate=cost(10**6, 4 * activations.size),
+        )(owner_table, part, *picked)
+    joined = pl.pallas_call(
+        join_kernel,
+        out_shape=jax.ShapeDtypeStruct((2 * tokens, width), outgoing.dtype),
+        in_specs=[VMEM] * 2,
+        out_specs=VMEM,
+        compiler_params=PARAMS,
+        cost_estimate=cost(10**6, 4 * outgoing.size),
+    )(outgoing, grads_other)
+    grads = {0: [relayed(joined, [(a, a) for a in range(replicas)])]}
+    acts = {0: picked[0]}
+    for gap in range(1, count):
+        acts[gap] = along(picked[gap], line_route(count, range(count - gap), 0, gap))
+    middle = None
+    for name, origins, start, gap in line_hops(count):
+        route = line_route(count, origins, start, gap)
+        if start:
+            piece = along(middle, route)
+        else:
+            piece = relayed(joined, route)
+        middle = piece if name == "far" else middle
+        grads.setdefault(gap, []).append(piece)
+    pieces, terms = [acts[0], *grads[0]], [(0, (1,))]
+    for gap in range(1, count):
+        for mirrored in (False, True):
+            group = [acts[gap], *grads[gap]]
+            if mirrored:
+                group = [swap(piece) for piece in group]
+            first = len(pieces)
+            terms.append((first, tuple(range(first + 1, first + len(group)))))
+            pieces += group
+    own = pl.pallas_call(
+        functools.partial(update_kernel, tuple(terms)),
+        out_shape=[jax.ShapeDtypeStruct((BLK // 2, width), jnp.bfloat16)] * 2,
+        in_specs=[VMEM] * len(pieces),
+        out_specs=[VMEM] * 2,
+        compiler_params=PARAMS,
+        cost_estimate=cost(27 * BLK * BLK * width, 2**20),
+    )(*pieces)
+    pieces, jobs = list(own), [(range(count), 0, 0), (range(count), 0, 1)]
+    for part in range(2):
+        middle = None
+        for name, origins, start, gap in line_hops(count):
+            route = line_route(count, origins, start, gap)
+            came = along(middle if start else own[part], route)
+            middle = came if name == "far" else middle
+            pieces += [came, swap(came)]
+            jobs.append((origins, gap, part))
+    result = pl.pallas_call(
+        functools.partial(place_kernel, count, tuple(jobs)),
+        out_shape=jax.ShapeDtypeStruct((count, BLK, width), jnp.bfloat16),
+        in_specs=[VMEM] * len(pieces),
+        out_specs=IN_HBM,
+        scratch_shapes=[pltpu.SemaphoreType.DMA((len(pieces),))],
+        compiler_params=PARAMS,
+        cost_estimate=cost(10**6, 2 * count * BLK * width),
+    )(*pieces)
+    return result[None]
+
+
+def body(owner_table, hidden_acts, sent_grad):
+    if lax.axis_size("dp") != 2 * owner_table.shape[1]:
+        return shards(owner_table, hidden_acts, sent_grad)
+    return pair_shards(owner_table, hidden_acts, sent_grad)
+
+
 def solution(mesh):
     return jax.shard_map(
-        shards,
+        body,
         mesh=mesh,
         in_specs=(P("section", None), P("section", "dp", None), P("section", "dp", None)),
         out_specs=P("section", None, None, None),

time: 116 us -> 80.4 us (0.69)
  the two profiles are of different devices: /device:TPU:0 before, /device:TPU:27 now
where the time goes in v1:
time: 80.4 us; the launch traced here: 80 us
  starting transfers between devices  63.9 us (79%)
  Pallas kernels  7.85 us (10%)
  waiting for transfers between devices  5.31 us (7%)
  local copies, waits for them, and re-layouts  2.6 us (3%)
    ppermute x17, starting transfers between devices, swap(): return lax.ppermute(piece, 'dp', swap_route)  39.3 us
    ppermute x12, starting transfers between devices, along(): return lax.ppermute(piece, 'dp', route)  17.7 us
    ppermute x4, starting transfers between devices, relayed(): return lax.ppermute(piece, ('section', 'dp'), pairs)  6.9 us
    pallas_call x1, Pallas kernels, pair_shards(): pl.pallas_call(functools.partial(update_kernel, tuple(terms)), out_shape=...  5.19 us
    ppermute x17, waiting for transfers between devices, swap(): return lax.ppermute(piece, 'dp', swap_route)  3.87 us
    unnamed x6, local copies, waits for them, and re-layouts  2.6 us
  transfers between devices with their start and end apart: 33, of which 5 were waited for; matrix products, arithmetic and copies ran while one was open for 0% of the time, Pallas kernels for 1%

profile of v1, /device:TPU:27, one launch (start us, length us, event | category | flops | bytes accessed | tf_op | source)
XLA Modules:
  0.0 80.0 jit_solution(5371182338787308326)
XLA Ops:
  0.0 0.7 collective-permute-start.1
  0.7 1.2 %collective-permute-done.1.high = bf16[128,512]{1,0:T(8,128)(2,1)S(1)} collective-permute-done((bf16[128,512]{1,0:T(8,128)(2,1)}, bf16[128,512]{1,0:T(8,128)(2,1)S(1)}, u32[]{:S(2)}, u32[]{:S(2)}) %collective-permute-start.1) | collective-permute-done | bytes 131104 | tf_op jit(solution)/shard_map/ppermute | solution.py:237
  1.9 0.9 %copy-done.1 = bf16[1,128,512]{2,1,0:T(8,128)(2,1)S(1)} copy-done((bf16[1,128,512]{2,1,0:T(8,128)(2,1)S(1)}, bf16[1,128,512]{2,1,0:T(8,128)(2,1)}, u32[]{:S(2)}) %copy-start.1) | copy-done | bytes 131096
  2.8 0.7 collective-permute-start.9
  3.5 1.9 %collective-permute-start.8 = (bf16[256,512]{1,0:T(8,128)(2,1)S(1)}, bf16[256,512]{1,0:T(8,128)(2,1)S(1)}, u32[]{:S(2)}, u32[]{:S(2)}) collective-permute-start(bf16[256,512]{1,0:T(8,128)(2,1)S(1)} %shard_map.39), channel_id=1, source_target_pairs={{8,4},{15,3},{16,12},{23,11},{24,20},{31,19},{0,28},{7,27}} | collective-permute-start | bytes 786440 | tf_op jit(solution)/shard_map/ppermute | solution.py:248
  5.4 4.0 %collective-permute-start.4 = (bf16[256,512]{1,0:T(8,128)(2,1)S(1)}, bf16[256,512]{1,0:T(8,128)(2,1)S(1)}, u32[]{:S(2)}, u32[]{:S(2)}) collective-permute-start(bf16[256,512]{1,0:T(8,128)(2,1)S(1)} %shard_map.39), channel_id=1, source_target_pairs={{8,2},{10,4},{12,6},{15,5},{13,3},{11,1},{16,10},{18,12},{20,14},{... | collective-permute-start | bytes 786440 | tf_op jit(solution)/shard_map/ppermute | solution.py:248
  9.4 0.3 collective-permute-start.2
  9.7 7.3 %collective-permute-start.12 = (bf16[256,512]{1,0:T(8,128)(2,1)S(1)}, bf16[256,512]{1,0:T(8,128)(2,1)S(1)}, u32[]{:S(2)}, u32[]{:S(2)}) collective-permute-start(bf16[256,512]{1,0:T(8,128)(2,1)S(1)} %collective-permute-done.9.refs_8_), channel_id=1, source_target_pairs={{0,1},{1,0},{2,3},{3,2},{4,5},{5,4},{6,7},{7,6},{8,9},{9,8},{10,11... | collective-permute-start | bytes 786440 | tf_op jit(solution)/shard_map/ppermute | solution.py:237
  17.0 1.0 %copy-done = bf16[1,128,2048]{2,1,0:T(8,128)(2,1)S(1)} copy-done((bf16[1,128,2048]{2,1,0:T(8,128)(2,1)S(1)}, bf16[1,128,2048]{2,1,0:T(8,128)(2,1)}, u32[]{:S(2)}) %copy-start) | copy-done | bytes 524312
  18.1 0.7 copy-done.2
  18.7 0.6 shard_map.37
  19.3 0.7 collective-permute-start.14
  20.0 0.0 collective-permute-done.acts
  20.0 0.7 collective-permute-start.11
  20.7 0.6 shard_map.38
  21.3 4.3 %collective-permute-start.3 = (bf16[256,512]{1,0:T(8,128)(2,1)S(1)}, bf16[256,512]{1,0:T(8,128)(2,1)S(1)}, u32[]{:S(2)}, u32[]{:S(2)}) collective-permute-start(bf16[256,512]{1,0:T(8,128)(2,1)S(1)} %get-tuple-element.20), channel_id=1, source_target_pairs={{0,2},{2,4},{4,6},{7,5},{5,3},{3,1},{8,10},{10,12},{12,14},{15,13}... | collective-permute-start | bytes 786440 | tf_op jit(solution)/shard_map/ppermute | solution.py:240
  25.6 0.0 collective-permute-done.2.refs_1_
  25.6 1.3 %collective-permute-start.7 = (bf16[256,512]{1,0:T(8,128)(2,1)S(1)}, bf16[256,512]{1,0:T(8,128)(2,1)S(1)}, u32[]{:S(2)}, u32[]{:S(2)}) collective-permute-start(bf16[256,512]{1,0:T(8,128)(2,1)S(1)} %get-tuple-element.21), channel_id=1, source_target_pairs={{0,4},{2,6},{7,3},{5,1},{8,12},{10,14},{15,11},{13,9},{16,20},{18,... | collective-permute-start | bytes 786440 | tf_op jit(solution)/shard_map/ppermute | solution.py:240
  27.0 0.0 collective-permute-done.12.refs_11_
  27.0 1.3 %collective-permute-start.13 = (bf16[256,512]{1,0:T(8,128)(2,1)S(1)}, bf16[256,512]{1,0:T(8,128)(2,1)S(1)}, u32[]{:S(2)}, u32[]{:S(2)}) collective-permute-start(bf16[256,512]{1,0:T(8,128)(2,1)S(1)} %get-tuple-element.22), channel_id=1, source_target_pairs={{0,6},{7,1},{8,14},{15,9},{16,22},{23,17},{24,30},{31,25}} | collective-permute-start | bytes 786440 | tf_op jit(solution)/shard_map/ppermute | solution.py:240
  28.3 0.0 collective-permute-done.14.refs_13_
  28.3 0.1 collective-permute-start.6
  28.4 0.0 collective-permute-done.11.refs_10_
  28.4 0.5 collective-permute-start.16
  28.9 0.0 collective-permute-done.3.refs_2_
  28.9 1.5 %collective-permute-start.5 = (bf16[256,512]{1,0:T(8,128)(2,1)S(1)}, bf16[256,512]{1,0:T(8,128)(2,1)S(1)}, u32[]{:S(2)}, u32[]{:S(2)}) collective-permute-start(bf16[256,512]{1,0:T(8,128)(2,1)S(1)} %collective-permute-done.3.refs_2_), channel_id=1, source_target_pairs={{0,1},{1,0},{2,3},{3,2},{4,5},{5,4},{6,7},{7,6},{8,9},{9,8},{10,11... | collective-permute-start | bytes 786440 | tf_op jit(solution)/shard_map/ppermute | solution.py:237
  30.4 1.4 %collective-permute-done.7.refs_6_ = bf16[256,512]{1,0:T(8,128)(2,1)S(1)} collective-permute-done((bf16[256,512]{1,0:T(8,128)(2,1)S(1)}, bf16[256,512]{1,0:T(8,128)(2,1)S(1)}, u32[]{:S(2)}, u32[]{:S(2)}) %collective-permute-start.7) | collective-permute-done | bytes 262176 | tf_op jit(solution)/shard_map/ppermute | solution.py:240
  31.8 8.4 %collective-permute-start.10 = (bf16[256,512]{1,0:T(8,128)(2,1)S(1)}, bf16[256,512]{1,0:T(8,128)(2,1)S(1)}, u32[]{:S(2)}, u32[]{:S(2)}) collective-permute-start(bf16[256,512]{1,0:T(8,128)(2,1)S(1)} %collective-permute-done.7.refs_6_), channel_id=1, source_target_pairs={{0,1},{1,0},{2,3},{3,2},{4,5},{5,4},{6,7},{7,6},{8,9},{9,8},{10,11... | collective-permute-start | bytes 786440 | tf_op jit(solution)/shard_map/ppermute | solution.py:237
  40.1 0.0 collective-permute-done.13.refs_12_
  40.1 0.0 collective-permute-start.15
  40.1 0.0 collective-permute-done.6.refs_5_
  40.2 0.0 collective-permute-done.5.refs_4_
  40.2 1.1 %collective-permute-done.10.refs_9_ = bf16[256,512]{1,0:T(8,128)(2,1)S(1)} collective-permute-done((bf16[256,512]{1,0:T(8,128)(2,1)S(1)}, bf16[256,512]{1,0:T(8,128)(2,1)S(1)}, u32[]{:S(2)}, u32[]{:S(2)}) %collective-permute-start.10) | collective-permute-done | bytes 262176 | tf_op jit(solution)/shard_map/ppermute | solution.py:237
  41.3 0.4 collective-permute-done.15.refs_14_
  41.7 5.2 %shard_map.40 = (bf16[256,512]{1,0:T(8,128)(2,1)S(1)}, bf16[256,512]{1,0:T(8,128)(2,1)S(1)}) custom-call(bf16[256,512]{1,0:T(8,128)(2,1)S(1)} %get-tuple-element.19.refs_0_, bf16[256,512]{1,0:T(8,128)(2,1)S(1)} %collective-permute-done.2.refs_1_, bf16[256,512]{1,0:T(8,128)(2,1)S(1)} %collective-permute-done.3.refs_2_, ...), custom_call_target="tpu_custom_call" | custom-call | flops 3623878656 | bytes 1048576 | tf_op jit(solution)/shard_map/pallas_call | solution.py:297
  46.9 1.3 %collective-permute-start.21 = (bf16[256,512]{1,0:T(8,128)(2,1)S(1)}, bf16[256,512]{1,0:T(8,128)(2,1)S(1)}, u32[]{:S(2)}, u32[]{:S(2)}) collective-permute-start(bf16[256,512]{1,0:T(8,128)(2,1)S(1)} %get-tuple-element.23.refs_0_), channel_id=1, source_target_pairs={{0,2},{2,4},{4,6},{7,5},{5,3},{3,1},{8,10},{10,12},{12,14},{15,13}... | collective-permute-start | bytes 786440 | tf_op jit(solution)/shard_map/ppermute | solution.py:240
  48.2 0.7 collective-permute-start.19
  48.9 2.9 %collective-permute-start.17 = (bf16[256,512]{1,0:T(8,128)(2,1)S(1)}, bf16[256,512]{1,0:T(8,128)(2,1)S(1)}, u32[]{:S(2)}, u32[]{:S(2)}) collective-permute-start(bf16[256,512]{1,0:T(8,128)(2,1)S(1)} %get-tuple-element.23.refs_0_), channel_id=1, source_target_pairs={{0,4},{7,3},{8,12},{15,11},{16,20},{23,19},{24,28},{31,27}} | collective-permute-start | bytes 786440 | tf_op jit(solution)/shard_map/ppermute | solution.py:240
  51.8 1.3 %collective-permute-start.29 = (bf16[256,512]{1,0:T(8,128)(2,1)S(1)}, bf16[256,512]{1,0:T(8,128)(2,1)S(1)}, u32[]{:S(2)}, u32[]{:S(2)}) collective-permute-start(bf16[256,512]{1,0:T(8,128)(2,1)S(1)} %get-tuple-element.24.refs_1_), channel_id=1, source_target_pairs={{0,2},{2,4},{4,6},{7,5},{5,3},{3,1},{8,10},{10,12},{12,14},{15,13}... | collective-permute-start | bytes 786440 | tf_op jit(solution)/shard_map/ppermute | solution.py:240
  53.1 0.7 collective-permute-start.27
  53.8 0.0 collective-permute-done.21.refs_6_
  53.8 1.9 %collective-permute-start.25 = (bf16[256,512]{1,0:T(8,128)(2,1)S(1)}, bf16[256,512]{1,0:T(8,128)(2,1)S(1)}, u32[]{:S(2)}, u32[]{:S(2)}) collective-permute-start(bf16[256,512]{1,0:T(8,128)(2,1)S(1)} %get-tuple-element.24.refs_1_), channel_id=1, source_target_pairs={{0,4},{7,3},{8,12},{15,11},{16,20},{23,19},{24,28},{31,27}} | collective-permute-start | bytes 786440 | tf_op jit(solution)/shard_map/ppermute | solution.py:240
  55.7 0.0 collective-permute-done.19.refs_4_
  55.7 3.3 %collective-permute-start.22 = (bf16[256,512]{1,0:T(8,128)(2,1)S(1)}, bf16[256,512]{1,0:T(8,128)(2,1)S(1)}, u32[]{:S(2)}, u32[]{:S(2)}) collective-permute-start(bf16[256,512]{1,0:T(8,128)(2,1)S(1)} %collective-permute-done.21.refs_6_), channel_id=1, source_target_pairs={{0,1},{1,0},{2,3},{3,2},{4,5},{5,4},{6,7},{7,6},{8,9},{9,8},{10,11... | collective-permute-start | bytes 786440 | tf_op jit(solution)/shard_map/ppermute | solution.py:237
  59.1 0.0 collective-permute-done.17.refs_2_
  59.1 0.1 collective-permute-start.20
  59.2 0.0 collective-permute-done.29.refs_14_
  59.2 0.7 collective-permute-start.23
  59.8 0.0 collective-permute-done.27.refs_12_
  59.9 9.2 %collective-permute-start.18 = (bf16[256,512]{1,0:T(8,128)(2,1)S(1)}, bf16[256,512]{1,0:T(8,128)(2,1)S(1)}, u32[]{:S(2)}, u32[]{:S(2)}) collective-permute-start(bf16[256,512]{1,0:T(8,128)(2,1)S(1)} %collective-permute-done.17.refs_2_), channel_id=1, source_target_pairs={{0,1},{1,0},{2,3},{3,2},{4,5},{5,4},{6,7},{7,6},{8,9},{9,8},{10,11... | collective-permute-start | bytes 786440 | tf_op jit(solution)/shard_map/ppermute | solution.py:237
  69.1 0.7 collective-permute-start.31
  69.8 0.0 collective-permute-done.22.refs_7_
  69.8 0.7 collective-permute-start.26
  70.5 0.1 collective-permute-start.30
  70.6 1.2 %collective-permute-start.28 = (bf16[256,512]{1,0:T(8,128)(2,1)S(1)}, bf16[256,512]{1,0:T(8,128)(2,1)S(1)}, u32[]{:S(2)}, u32[]{:S(2)}) collective-permute-start(bf16[256,512]{1,0:T(8,128)(2,1)S(1)} %collective-permute-done.27.refs_12_), channel_id=1, source_target_pairs={{0,1},{1,0},{2,3},{3,2},{4,5},{5,4},{6,7},{7,6},{8,9},{9,8},{10,11... | collective-permute-start | bytes 786440 | tf_op jit(solution)/shard_map/ppermute | solution.py:237
  71.8 0.0 collective-permute-start.24
  71.8 0.0 collective-permute-done.31.refs_16_
  71.8 5.5 %collective-permute-start.32 = (bf16[256,512]{1,0:T(8,128)(2,1)S(1)}, bf16[256,512]{1,0:T(8,128)(2,1)S(1)}, u32[]{:S(2)}, u32[]{:S(2)}) collective-permute-start(bf16[256,512]{1,0:T(8,128)(2,1)S(1)} %collective-permute-done.31.refs_16_), channel_id=1, source_target_pairs={{0,1},{1,0},{2,3},{3,2},{4,5},{5,4},{6,7},{7,6},{8,9},{9,8},{10,11... | collective-permute-start | bytes 786440 | tf_op jit(solution)/shard_map/ppermute | solution.py:237
  77.4 0.0 collective-permute-done.30.refs_15_
  77.4 0.0 collective-permute-done.28.refs_13_
  77.4 0.0 collective-permute-done.26.refs_11_
  77.4 0.0 collective-permute-done.24.refs_9_
  77.4 1.1 %collective-permute-done.32.refs_17_ = bf16[256,512]{1,0:T(8,128)(2,1)S(1)} collective-permute-done((bf16[256,512]{1,0:T(8,128)(2,1)S(1)}, bf16[256,512]{1,0:T(8,128)(2,1)S(1)}, u32[]{:S(2)}, u32[]{:S(2)}) %collective-permute-start.32) | collective-permute-done | bytes 262176 | tf_op jit(solution)/shard_map/ppermute | solution.py:237
  78.5 1.5 %shard_map.41 = bf16[4,512,512]{2,1,0:T(8,128)(2,1)} custom-call(bf16[256,512]{1,0:T(8,128)(2,1)S(1)} %get-tuple-element.23.refs_0_, bf16[256,512]{1,0:T(8,128)(2,1)S(1)} %get-tuple-element.24.refs_1_, bf16[256,512]{1,0:T(8,128)(2,1)S(1)} %collective-permute-done.17.refs_2_, bf16[256,512]{1,0:T(8,128)(2,1)S(1)} %collective-permute-done.18.refs_3_, ...), custom_call_target="tpu_custom_call" | custom-call | flops 1000000 | bytes 2097152 | tf_op jit(solution)/shard_map/pallas_call | solution.py:314
  (13 shorter events, 0.0 us)
Async XLA Ops:
  0.0 1.9 %collective-permute-start.1 = (bf16[128,512]{1,0:T(8,128)(2,1)}, bf16[128,512]{1,0:T(8,128)(2,1)S(1)}, u32[]{:S(2)}, u32[]{:S(2)}) collective-permute-start(bf16[128,512]{1,0:T(8,128)(2,1)} %bitcast.5), channel_id=1, source_target_pairs={{0,1},{1,0},{2,3},{3,2},{4,5},{5,4},{6,7},{7,6},{8,9},{9,8},{10,11... | collective-permute-start | bytes 393224 | tf_op jit(solution)/shard_map/ppermute | solution.py:237
  0.7 19.4 %collective-permute-start = (bf16[128,2048]{1,0:T(8,128)(2,1)}, bf16[128,2048]{1,0:T(8,128)(2,1)S(1)}, u32[]{:S(2)}, u32[]{:S(2)}) collective-permute-start(bf16[128,2048]{1,0:T(8,128)(2,1)} %bitcast.3), channel_id=1, source_target_pairs={{0,1},{1,0},{2,3},{3,2},{4,5},{5,4},{6,7},{7,6},{8,9},{9,8},{10,11... | collective-permute-start | bytes 1572872 | tf_op jit(solution)/shard_map/ppermute | solution.py:237
  1.9 0.9 %copy-start.1 = (bf16[1,128,512]{2,1,0:T(8,128)(2,1)S(1)}, bf16[1,128,512]{2,1,0:T(8,128)(2,1)}, u32[]{:S(2)}) copy-start(bf16[1,128,512]{2,1,0:T(8,128)(2,1)} %param.5) | copy-start | bytes 393220
  2.8 6.9 %collective-permute-start.9 = (bf16[256,512]{1,0:T(8,128)(2,1)S(1)}, bf16[256,512]{1,0:T(8,128)(2,1)S(1)}, u32[]{:S(2)}, u32[]{:S(2)}) collective-permute-start(bf16[256,512]{1,0:T(8,128)(2,1)S(1)} %shard_map.39), channel_id=1, source_target_pairs={{10,6},{13,1},{18,14},{21,9},{26,22},{29,17},{2,30},{5,25}} | collective-permute-start | bytes 786440 | tf_op jit(solution)/shard_map/ppermute | solution.py:248
  3.5 15.8 %collective-permute-start.8 = (bf16[256,512]{1,0:T(8,128)(2,1)S(1)}, bf16[256,512]{1,0:T(8,128)(2,1)S(1)}, u32[]{:S(2)}, u32[]{:S(2)}) collective-permute-start(bf16[256,512]{1,0:T(8,128)(2,1)S(1)} %shard_map.39), channel_id=1, source_target_pairs={{8,4},{15,3},{16,12},{23,11},{24,20},{31,19},{0,28},{7,27}} | collective-permute-start | bytes 786440 | tf_op jit(solution)/shard_map/ppermute | solution.py:248
  5.4 15.9 %collective-permute-start.4 = (bf16[256,512]{1,0:T(8,128)(2,1)S(1)}, bf16[256,512]{1,0:T(8,128)(2,1)S(1)}, u32[]{:S(2)}, u32[]{:S(2)}) collective-permute-start(bf16[256,512]{1,0:T(8,128)(2,1)S(1)} %shard_map.39), channel_id=1, source_target_pairs={{8,2},{10,4},{12,6},{15,5},{13,3},{11,1},{16,10},{18,12},{20,14},{... | collective-permute-start | bytes 786440 | tf_op jit(solution)/shard_map/ppermute | solution.py:248
  9.4 16.2 %collective-permute-start.2 = (bf16[256,512]{1,0:T(8,128)(2,1)S(1)}, bf16[256,512]{1,0:T(8,128)(2,1)S(1)}, u32[]{:S(2)}, u32[]{:S(2)}) collective-permute-start(bf16[256,512]{1,0:T(8,128)(2,1)S(1)} %shard_map.39), channel_id=1, source_target_pairs={{8,0},{9,1},{10,2},{11,3},{12,4},{13,5},{14,6},{15,7},{16,8},{17,9... | collective-permute-start | bytes 786440 | tf_op jit(solution)/shard_map/ppermute | solution.py:248
  9.7 17.2 %collective-permute-start.12 = (bf16[256,512]{1,0:T(8,128)(2,1)S(1)}, bf16[256,512]{1,0:T(8,128)(2,1)S(1)}, u32[]{:S(2)}, u32[]{:S(2)}) collective-permute-start(bf16[256,512]{1,0:T(8,128)(2,1)S(1)} %collective-permute-done.9.refs_8_), channel_id=1, source_target_pairs={{0,1},{1,0},{2,3},{3,2},{4,5},{5,4},{6,7},{7,6},{8,9},{9,8},{10,11... | collective-permute-start | bytes 786440 | tf_op jit(solution)/shard_map/ppermute | solution.py:237
  17.0 1.0 %copy-start = (bf16[1,128,2048]{2,1,0:T(8,128)(2,1)S(1)}, bf16[1,128,2048]{2,1,0:T(8,128)(2,1)}, u32[]{:S(2)}) copy-start(bf16[1,128,2048]{2,1,0:T(8,128)(2,1)} %param.4) | copy-start | bytes 1572868
  18.1 0.7 copy-start.2
  19.3 8.9 %collective-permute-start.14 = (bf16[256,512]{1,0:T(8,128)(2,1)S(1)}, bf16[256,512]{1,0:T(8,128)(2,1)S(1)}, u32[]{:S(2)}, u32[]{:S(2)}) collective-permute-start(bf16[256,512]{1,0:T(8,128)(2,1)S(1)} %collective-permute-done.8.refs_7_), channel_id=1, source_target_pairs={{4,6},{3,1},{12,14},{11,9},{20,22},{19,17},{28,30},{27,25}} | collective-permute-start | bytes 786440 | tf_op jit(solution)/shard_map/ppermute | solution.py:240
  20.0 8.3 %collective-permute-start.11 = (bf16[256,512]{1,0:T(8,128)(2,1)S(1)}, bf16[256,512]{1,0:T(8,128)(2,1)S(1)}, u32[]{:S(2)}, u32[]{:S(2)}) collective-permute-start(bf16[256,512]{1,0:T(8,128)(2,1)S(1)} %collective-permute-done.8.refs_7_), channel_id=1, source_target_pairs={{0,1},{1,0},{2,3},{3,2},{4,5},{5,4},{6,7},{7,6},{8,9},{9,8},{10,11... | collective-permute-start | bytes 786440 | tf_op jit(solution)/shard_map/ppermute | solution.py:237
  21.3 7.6 %collective-permute-start.3 = (bf16[256,512]{1,0:T(8,128)(2,1)S(1)}, bf16[256,512]{1,0:T(8,128)(2,1)S(1)}, u32[]{:S(2)}, u32[]{:S(2)}) collective-permute-start(bf16[256,512]{1,0:T(8,128)(2,1)S(1)} %get-tuple-element.20), channel_id=1, source_target_pairs={{0,2},{2,4},{4,6},{7,5},{5,3},{3,1},{8,10},{10,12},{12,14},{15,13}... | collective-permute-start | bytes 786440 | tf_op jit(solution)/shard_map/ppermute | solution.py:240
  25.6 6.1 %collective-permute-start.7 = (bf16[256,512]{1,0:T(8,128)(2,1)S(1)}, bf16[256,512]{1,0:T(8,128)(2,1)S(1)}, u32[]{:S(2)}, u32[]{:S(2)}) collective-permute-start(bf16[256,512]{1,0:T(8,128)(2,1)S(1)} %get-tuple-element.21), channel_id=1, source_target_pairs={{0,4},{2,6},{7,3},{5,1},{8,12},{10,14},{15,11},{13,9},{16,20},{18,... | collective-permute-start | bytes 786440 | tf_op jit(solution)/shard_map/ppermute | solution.py:240
  27.0 13.2 %collective-permute-start.13 = (bf16[256,512]{1,0:T(8,128)(2,1)S(1)}, bf16[256,512]{1,0:T(8,128)(2,1)S(1)}, u32[]{:S(2)}, u32[]{:S(2)}) collective-permute-start(bf16[256,512]{1,0:T(8,128)(2,1)S(1)} %get-tuple-element.22), channel_id=1, source_target_pairs={{0,6},{7,1},{8,14},{15,9},{16,22},{23,17},{24,30},{31,25}} | collective-permute-start | bytes 786440 | tf_op jit(solution)/shard_map/ppermute | solution.py:240
  28.3 11.9 %collective-permute-start.6 = (bf16[256,512]{1,0:T(8,128)(2,1)S(1)}, bf16[256,512]{1,0:T(8,128)(2,1)S(1)}, u32[]{:S(2)}, u32[]{:S(2)}) collective-permute-start(bf16[256,512]{1,0:T(8,128)(2,1)S(1)} %collective-permute-done.4.refs_3_), channel_id=1, source_target_pairs={{0,1},{1,0},{2,3},{3,2},{4,5},{5,4},{6,7},{7,6},{8,9},{9,8},{10,11... | collective-permute-start | bytes 786440 | tf_op jit(solution)/shard_map/ppermute | solution.py:237
  28.4 11.8 %collective-permute-start.16 = (bf16[256,512]{1,0:T(8,128)(2,1)S(1)}, bf16[256,512]{1,0:T(8,128)(2,1)S(1)}, u32[]{:S(2)}, u32[]{:S(2)}) collective-permute-start(bf16[256,512]{1,0:T(8,128)(2,1)S(1)} %collective-permute-done.14.refs_13_), channel_id=1, source_target_pairs={{0,1},{1,0},{2,3},{3,2},{4,5},{5,4},{6,7},{7,6},{8,9},{9,8},{10,11... | collective-permute-start | bytes 786440 | tf_op jit(solution)/shard_map/ppermute | solution.py:237
  28.9 11.2 %collective-permute-start.5 = (bf16[256,512]{1,0:T(8,128)(2,1)S(1)}, bf16[256,512]{1,0:T(8,128)(2,1)S(1)}, u32[]{:S(2)}, u32[]{:S(2)}) collective-permute-start(bf16[256,512]{1,0:T(8,128)(2,1)S(1)} %collective-permute-done.3.refs_2_), channel_id=1, source_target_pairs={{0,1},{1,0},{2,3},{3,2},{4,5},{5,4},{6,7},{7,6},{8,9},{9,8},{10,11... | collective-permute-start | bytes 786440 | tf_op jit(solution)/shard_map/ppermute | solution.py:237
  31.8 9.5 %collective-permute-start.10 = (bf16[256,512]{1,0:T(8,128)(2,1)S(1)}, bf16[256,512]{1,0:T(8,128)(2,1)S(1)}, u32[]{:S(2)}, u32[]{:S(2)}) collective-permute-start(bf16[256,512]{1,0:T(8,128)(2,1)S(1)} %collective-permute-done.7.refs_6_), channel_id=1, source_target_pairs={{0,1},{1,0},{2,3},{3,2},{4,5},{5,4},{6,7},{7,6},{8,9},{9,8},{10,11... | collective-permute-start | bytes 786440 | tf_op jit(solution)/shard_map/ppermute | solution.py:237
  40.1 1.5 %collective-permute-start.15 = (bf16[256,512]{1,0:T(8,128)(2,1)S(1)}, bf16[256,512]{1,0:T(8,128)(2,1)S(1)}, u32[]{:S(2)}, u32[]{:S(2)}) collective-permute-start(bf16[256,512]{1,0:T(8,128)(2,1)S(1)} %collective-permute-done.13.refs_12_), channel_id=1, source_target_pairs={{0,1},{1,0},{2,3},{3,2},{4,5},{5,4},{6,7},{7,6},{8,9},{9,8},{10,11... | collective-permute-start | bytes 786440 | tf_op jit(solution)/shard_map/ppermute | solution.py:237
  46.9 6.9 %collective-permute-start.21 = (bf16[256,512]{1,0:T(8,128)(2,1)S(1)}, bf16[256,512]{1,0:T(8,128)(2,1)S(1)}, u32[]{:S(2)}, u32[]{:S(2)}) collective-permute-start(bf16[256,512]{1,0:T(8,128)(2,1)S(1)} %get-tuple-element.23.refs_0_), channel_id=1, source_target_pairs={{0,2},{2,4},{4,6},{7,5},{5,3},{3,1},{8,10},{10,12},{12,14},{15,13}... | collective-permute-start | bytes 786440 | tf_op jit(solution)/shard_map/ppermute | solution.py:240
  48.2 7.5 %collective-permute-start.19 = (bf16[256,512]{1,0:T(8,128)(2,1)S(1)}, bf16[256,512]{1,0:T(8,128)(2,1)S(1)}, u32[]{:S(2)}, u32[]{:S(2)}) collective-permute-start(bf16[256,512]{1,0:T(8,128)(2,1)S(1)} %get-tuple-element.23.refs_0_), channel_id=1, source_target_pairs={{2,6},{5,1},{10,14},{13,9},{18,22},{21,17},{26,30},{29,25}} | collective-permute-start | bytes 786440 | tf_op jit(solution)/shard_map/ppermute | solution.py:240
  48.9 10.2 %collective-permute-start.17 = (bf16[256,512]{1,0:T(8,128)(2,1)S(1)}, bf16[256,512]{1,0:T(8,128)(2,1)S(1)}, u32[]{:S(2)}, u32[]{:S(2)}) collective-permute-start(bf16[256,512]{1,0:T(8,128)(2,1)S(1)} %get-tuple-element.23.refs_0_), channel_id=1, source_target_pairs={{0,4},{7,3},{8,12},{15,11},{16,20},{23,19},{24,28},{31,27}} | collective-permute-start | bytes 786440 | tf_op jit(solution)/shard_map/ppermute | solution.py:240
  51.8 7.4 %collective-permute-start.29 = (bf16[256,512]{1,0:T(8,128)(2,1)S(1)}, bf16[256,512]{1,0:T(8,128)(2,1)S(1)}, u32[]{:S(2)}, u32[]{:S(2)}) collective-permute-start(bf16[256,512]{1,0:T(8,128)(2,1)S(1)} %get-tuple-element.24.refs_1_), channel_id=1, source_target_pairs={{0,2},{2,4},{4,6},{7,5},{5,3},{3,1},{8,10},{10,12},{12,14},{15,13}... | collective-permute-start | bytes 786440 | tf_op jit(solution)/shard_map/ppermute | solution.py:240
  53.1 6.7 %collective-permute-start.27 = (bf16[256,512]{1,0:T(8,128)(2,1)S(1)}, bf16[256,512]{1,0:T(8,128)(2,1)S(1)}, u32[]{:S(2)}, u32[]{:S(2)}) collective-permute-start(bf16[256,512]{1,0:T(8,128)(2,1)S(1)} %get-tuple-element.24.refs_1_), channel_id=1, source_target_pairs={{2,6},{5,1},{10,14},{13,9},{18,22},{21,17},{26,30},{29,25}} | collective-permute-start | bytes 786440 | tf_op jit(solution)/shard_map/ppermute | solution.py:240
  53.8 15.3 %collective-permute-start.25 = (bf16[256,512]{1,0:T(8,128)(2,1)S(1)}, bf16[256,512]{1,0:T(8,128)(2,1)S(1)}, u32[]{:S(2)}, u32[]{:S(2)}) collective-permute-start(bf16[256,512]{1,0:T(8,128)(2,1)S(1)} %get-tuple-element.24.refs_1_), channel_id=1, source_target_pairs={{0,4},{7,3},{8,12},{15,11},{16,20},{23,19},{24,28},{31,27}} | collective-permute-start | bytes 786440 | tf_op jit(solution)/shard_map/ppermute | solution.py:240
  55.7 14.0 %collective-permute-start.22 = (bf16[256,512]{1,0:T(8,128)(2,1)S(1)}, bf16[256,512]{1,0:T(8,128)(2,1)S(1)}, u32[]{:S(2)}, u32[]{:S(2)}) collective-permute-start(bf16[256,512]{1,0:T(8,128)(2,1)S(1)} %collective-permute-done.21.refs_6_), channel_id=1, source_target_pairs={{0,1},{1,0},{2,3},{3,2},{4,5},{5,4},{6,7},{7,6},{8,9},{9,8},{10,11... | collective-permute-start | bytes 786440 | tf_op jit(solution)/shard_map/ppermute | solution.py:237
  59.1 11.4 %collective-permute-start.20 = (bf16[256,512]{1,0:T(8,128)(2,1)S(1)}, bf16[256,512]{1,0:T(8,128)(2,1)S(1)}, u32[]{:S(2)}, u32[]{:S(2)}) collective-permute-start(bf16[256,512]{1,0:T(8,128)(2,1)S(1)} %collective-permute-done.19.refs_4_), channel_id=1, source_target_pairs={{0,1},{1,0},{2,3},{3,2},{4,5},{5,4},{6,7},{7,6},{8,9},{9,8},{10,11... | collective-permute-start | bytes 786440 | tf_op jit(solution)/shard_map/ppermute | solution.py:237
  59.2 11.4 %collective-permute-start.23 = (bf16[256,512]{1,0:T(8,128)(2,1)S(1)}, bf16[256,512]{1,0:T(8,128)(2,1)S(1)}, u32[]{:S(2)}, u32[]{:S(2)}) collective-permute-start(bf16[256,512]{1,0:T(8,128)(2,1)S(1)} %collective-permute-done.17.refs_2_), channel_id=1, source_target_pairs={{4,6},{3,1},{12,14},{11,9},{20,22},{19,17},{28,30},{27,25}} | collective-permute-start | bytes 786440 | tf_op jit(solution)/shard_map/ppermute | solution.py:240
  59.9 12.0 %collective-permute-start.18 = (bf16[256,512]{1,0:T(8,128)(2,1)S(1)}, bf16[256,512]{1,0:T(8,128)(2,1)S(1)}, u32[]{:S(2)}, u32[]{:S(2)}) collective-permute-start(bf16[256,512]{1,0:T(8,128)(2,1)S(1)} %collective-permute-done.17.refs_2_), channel_id=1, source_target_pairs={{0,1},{1,0},{2,3},{3,2},{4,5},{5,4},{6,7},{7,6},{8,9},{9,8},{10,11... | collective-permute-start | bytes 786440 | tf_op jit(solution)/shard_map/ppermute | solution.py:237
  69.1 2.7 %collective-permute-start.31 = (bf16[256,512]{1,0:T(8,128)(2,1)S(1)}, bf16[256,512]{1,0:T(8,128)(2,1)S(1)}, u32[]{:S(2)}, u32[]{:S(2)}) collective-permute-start(bf16[256,512]{1,0:T(8,128)(2,1)S(1)} %collective-permute-done.25.refs_10_), channel_id=1, source_target_pairs={{4,6},{3,1},{12,14},{11,9},{20,22},{19,17},{28,30},{27,25}} | collective-permute-start | bytes 786440 | tf_op jit(solution)/shard_map/ppermute | solution.py:240
  69.8 7.6 %collective-permute-start.26 = (bf16[256,512]{1,0:T(8,128)(2,1)S(1)}, bf16[256,512]{1,0:T(8,128)(2,1)S(1)}, u32[]{:S(2)}, u32[]{:S(2)}) collective-permute-start(bf16[256,512]{1,0:T(8,128)(2,1)S(1)} %collective-permute-done.25.refs_10_), channel_id=1, source_target_pairs={{0,1},{1,0},{2,3},{3,2},{4,5},{5,4},{6,7},{7,6},{8,9},{9,8},{10,11... | collective-permute-start | bytes 786440 | tf_op jit(solution)/shard_map/ppermute | solution.py:237
  70.5 6.9 %collective-permute-start.30 = (bf16[256,512]{1,0:T(8,128)(2,1)S(1)}, bf16[256,512]{1,0:T(8,128)(2,1)S(1)}, u32[]{:S(2)}, u32[]{:S(2)}) collective-permute-start(bf16[256,512]{1,0:T(8,128)(2,1)S(1)} %collective-permute-done.29.refs_14_), channel_id=1, source_target_pairs={{0,1},{1,0},{2,3},{3,2},{4,5},{5,4},{6,7},{7,6},{8,9},{9,8},{10,11... | collective-permute-start | bytes 786440 | tf_op jit(solution)/shard_map/ppermute | solution.py:237
  70.6 6.8 %collective-permute-start.28 = (bf16[256,512]{1,0:T(8,128)(2,1)S(1)}, bf16[256,512]{1,0:T(8,128)(2,1)S(1)}, u32[]{:S(2)}, u32[]{:S(2)}) collective-permute-start(bf16[256,512]{1,0:T(8,128)(2,1)S(1)} %collective-permute-done.27.refs_12_), channel_id=1, source_target_pairs={{0,1},{1,0},{2,3},{3,2},{4,5},{5,4},{6,7},{7,6},{8,9},{9,8},{10,11... | collective-permute-start | bytes 786440 | tf_op jit(solution)/shard_map/ppermute | solution.py:237
  71.8 5.6 %collective-permute-start.24 = (bf16[256,512]{1,0:T(8,128)(2,1)S(1)}, bf16[256,512]{1,0:T(8,128)(2,1)S(1)}, u32[]{:S(2)}, u32[]{:S(2)}) collective-permute-start(bf16[256,512]{1,0:T(8,128)(2,1)S(1)} %collective-permute-done.23.refs_8_), channel_id=1, source_target_pairs={{0,1},{1,0},{2,3},{3,2},{4,5},{5,4},{6,7},{7,6},{8,9},{9,8},{10,11... | collective-permute-start | bytes 786440 | tf_op jit(solution)/shard_map/ppermute | solution.py:237
  71.8 6.7 %collective-permute-start.32 = (bf16[256,512]{1,0:T(8,128)(2,1)S(1)}, bf16[256,512]{1,0:T(8,128)(2,1)S(1)}, u32[]{:S(2)}, u32[]{:S(2)}) collective-permute-start(bf16[256,512]{1,0:T(8,128)(2,1)S(1)} %collective-permute-done.31.refs_16_), channel_id=1, source_target_pairs={{0,1},{1,0},{2,3},{3,2},{4,5},{5,4},{6,7},{7,6},{8,9},{9,8},{10,11... | collective-permute-start | bytes 786440 | tf_op jit(solution)/shard_map/ppermute | solution.py:237
